TPU v7x, 32 devices: a whole 2x2x4 slice. The times are simulated.
32 devices in a mesh: grp: 2 (over y), mem: 16 (over z, x, core).
Axes of the slice: x: 2, y: 2, z: 4, core: 2. Of those that a mesh axis runs over, the one named last changes fastest.
Arguments:
- tokens: bfloat16 [4096, 1024], P(('grp', 'mem')), may hold values from -6 to 6
- cotangent: bfloat16 [4096, 1024], P(('grp', 'mem')), may hold values from -6 to 6
- path: int32 [32, 3], P(('grp', 'mem')), may hold values from 0 to 63, as said below
- coarse_weights: bfloat16 [4, 1024, 512], P(None, 'mem'), may hold values from -0.1875 to 0.1875
- middle_weights: bfloat16 [64, 1024, 256], P(None, 'mem'), may hold values from -0.1875 to 0.1875
- fine_weights: bfloat16 [64, 1024, 128], P('grp', 'mem'), may hold values from -0.1875 to 0.1875
Outputs:
- tokens_grad: bfloat16 [4096, 1024], P(('grp', 'mem'))
- coarse_grad: bfloat16 [4, 1024, 512], P(None, 'mem')
- middle_grad: bfloat16 [64, 1024, 256], P(None, 'mem')
- fine_grad: bfloat16 [64, 1024, 128], P('grp', 'mem')
Inputs may be any that keep to these rules, and one draw needn't show every extreme that they name: Row d is the path of document d: column 0 its coarse block, column 1 its middle block, column 2 its fine block, with middle = fine * 1 and coarse = middle * 4 // 64. Some fine blocks are chosen by many documents.
All inputs are finite; a program needn't handle non-finite values.
Results may differ from a plain program's by a relative error of at most 0.005.
Values may be sent and summed in bfloat16 or wider, within the bound.
A program may use at most 64 MiB of HBM per device.

v0:
```python
from functools import partial

import jax
import jax.numpy as jnp
from jax import lax
from jax.sharding import PartitionSpec as P


def contract_rows(left, right):
    return lax.dot_general(
        left, right, (((0,), (0,)), ((), ())), preferred_element_type=jnp.float32
    )


def level_terms(inputs, upstream, weights):
    hidden_width = weights.shape[1] // 2
    up_half = weights[:, :hidden_width]
    down_half = weights[:, hidden_width:]
    before = jnp.dot(inputs, up_half, preferred_element_type=jnp.float32)
    hidden, pullback = jax.vjp(partial(jax.nn.gelu, approximate=True), before)
    hidden_low = hidden.astype(jnp.bfloat16)
    hidden_grad = jnp.dot(upstream, down_half, preferred_element_type=jnp.float32)
    before_grad = pullback(hidden_grad)[0].astype(jnp.bfloat16)
    up_grad = contract_rows(inputs, before_grad)
    down_grad = contract_rows(upstream, hidden_low)
    input_part = lax.dot_general(
        before_grad, up_half, (((1,), (1,)), ((), ())), preferred_element_type=jnp.float32
    )
    return (jnp.concatenate([up_grad, down_grad], axis=1), input_part)


def one_hot_rows(identity, count):
    return (identity[:, None] == jnp.arange(count, dtype=jnp.int32)[None, :]).astype(jnp.bfloat16)


def select_blocks(picker, blocks):
    return jnp.einsum("mk,krh->mrh", picker, blocks, preferred_element_type=jnp.float32).astype(
        jnp.bfloat16
    )


def collect_blocks(picker, pieces):
    return jnp.einsum(
        "mk,mrh->krh", picker.astype(jnp.float32), pieces, precision=lax.Precision.HIGHEST
    )


def on_device(tokens, cotangent, path, coarse_weights, middle_weights, fine_weights):
    member_count = lax.axis_size("mem")
    group_count = lax.axis_size("grp")
    group = lax.axis_index("grp")
    row_count = coarse_weights.shape[1]
    fine_owned = fine_weights.shape[0]
    route = path[0]
    all_paths = lax.all_gather(path, ("grp", "mem"), axis=0, tiled=True)
    group_paths = lax.dynamic_slice_in_dim(all_paths, group * member_count, member_count, 0)
    coarse_pick = one_hot_rows(group_paths[:, 0], coarse_weights.shape[0])
    middle_pick = one_hot_rows(group_paths[:, 1], middle_weights.shape[0])
    middle_send = select_blocks(middle_pick, middle_weights)
    every_block = lax.all_gather(coarse_weights, "mem", axis=1, tiled=True)
    coarse_block = lax.dynamic_index_in_dim(every_block, route[0], 0, keepdims=False)
    middle_block = lax.all_to_all(middle_send, "mem", split_axis=0, concat_axis=1, tiled=True)[0]
    offsets = all_paths[:, 2] - group * fine_owned
    fine_pick = one_hot_rows(offsets, fine_owned)
    fine_send = select_blocks(fine_pick, fine_weights).reshape(
        group_count, member_count, row_count, fine_weights.shape[2]
    )
    arrived = lax.all_to_all(fine_send, "grp", split_axis=0, concat_axis=0, tiled=True)
    merged = jnp.sum(arrived, axis=0, dtype=jnp.float32).astype(jnp.bfloat16)
    fine_block = lax.all_to_all(merged, "mem", split_axis=0, concat_axis=1, tiled=True)[0]
    coarse_term, coarse_back = level_terms(tokens, cotangent, coarse_block)
    middle_term, middle_back = level_terms(tokens, cotangent, middle_block)
    fine_term, fine_back = level_terms(tokens, cotangent, fine_block)
    tokens_grad = (coarse_back + middle_back + fine_back).astype(jnp.bfloat16)
    coarse_parts, middle_parts = (
        lax.all_to_all(
            coarse_term.reshape(member_count, row_count, -1),
            "mem",
            split_axis=0,
            concat_axis=0,
            tiled=True,
        ),
        lax.all_to_all(
            middle_term.reshape(member_count, row_count, -1),
            "mem",
            split_axis=0,
            concat_axis=0,
            tiled=True,
        ),
    )
    coarse_local = collect_blocks(coarse_pick, coarse_parts)
    middle_local = collect_blocks(middle_pick, middle_parts)
    coarse_total, middle_total = lax.psum((coarse_local, middle_local), "grp")
    fine_parts = lax.all_to_all(
        fine_term.reshape(member_count, row_count, -1),
        "mem",
        split_axis=0,
        concat_axis=0,
        tiled=True,
    )
    owner_group = group_paths[:, 2] // fine_owned
    destined = (jnp.arange(group_count, dtype=jnp.int32)[:, None] == owner_group[None, :]).astype(
        jnp.float32
    )
    outgoing = destined[:, :, None, None] * fine_parts[None]
    returned = lax.all_to_all(outgoing, "grp", split_axis=0, concat_axis=0, tiled=True)
    fine_local = collect_blocks(
        fine_pick, returned.reshape(group_count * member_count, row_count, -1)
    )
    return (
        tokens_grad,
        coarse_total.astype(jnp.bfloat16),
        middle_total.astype(jnp.bfloat16),
        fine_local.astype(jnp.bfloat16),
    )


def solution(mesh):
    return jax.shard_map(
        on_device,
        mesh=mesh,
        in_specs=(
            P(("grp", "mem"), None),
            P(("grp", "mem"), None),
            P(("grp", "mem"), None),
            P(None, "mem", None),
            P(None, "mem", None),
            P("grp", "mem", None),
        ),
        out_specs=(
            P(("grp", "mem"), None),
            P(None, "mem", None),
            P(None, "mem", None),
            P("grp", "mem", None),
        ),
        check_vma=False,
    )
```

profile of v0, /device:TPU:11, one launch (start us, length us, event | category | flops | bytes accessed | tf_op | source)
XLA Modules:
  0.0 344.5 jit_solution(11995340162909962336)
XLA Ops:
  7.2 0.0 copy-start
  7.2 0.0 all-gather.3.cloned.1.call-start
  7.2 0.7 all-gather.3.cloned.1.call-update
  7.9 34.2 %all-gather = s32[32,1,3]{2,1,0:T(1,128)S(1)} all-gather(s32[1,1,3]{2,1,0:T(1,128)} %bitcast.103), channel_id=1, replica_groups=mesh['grp'=2,'mem'=16] {'grp','mem'}, dimensions={0}, use_global_device_ids=true | all-gather | bytes 396 | tf_op jit(solution)/shard_map/all_gather | solution.py:55
  42.2 0.1 copy.76
  42.2 1.5 convolution_convert_fusion.1
  43.7 0.8 copy.79
  44.5 3.5 %all-to-all-start.1 = ((bf16[2,16,64,128]{3,1,2,0:T(8,128)(2,1)}), bf16[2,16,64,128]{3,1,2,0:T(8,128)(2,1)S(1)}, u32[]{:S(2)}, u32[]{:S(2)}) async-start(bf16[2,16,64,128]{3,1,2,0:T(8,128)(2,1)} %copy.79), calls=%async_computation.1 | async-start | bytes 1048576 | tf_op jit(solution)/shard_map/all_to_all | solution.py:68
  48.1 0.1 copy.73
  48.1 7.9 %all-to-all-done.1 = bf16[2,16,64,128]{3,1,2,0:T(8,128)(2,1)S(1)} async-done(((bf16[2,16,64,128]{3,1,2,0:T(8,128)(2,1)}), bf16[2,16,64,128]{3,1,2,0:T(8,128)(2,1)S(1)}, u32[]{:S(2)}, u32[]{:S(2)}) %all-to-all-start.1) | async-done | bytes 524320 | tf_op jit(solution)/shard_map/all_to_all | solution.py:68
  56.0 0.2 reduce_sum.12
  56.2 0.8 copy.81
  57.0 12.9 %all-to-all-start.2 = ((bf16[16,64,128]{2,1,0:T(8,128)(2,1)}), bf16[16,64,128]{2,1,0:T(8,128)(2,1)S(1)}, u32[]{:S(2)}, u32[]{:S(2)}) async-start(bf16[16,64,128]{2,1,0:T(8,128)(2,1)} %copy.81), calls=%async_computation.2 | async-start | bytes 524288 | tf_op jit(solution)/shard_map/all_to_all | solution.py:70
  69.9 0.0 copy-start.1
  69.9 0.0 copy-start.4
  69.9 1.2 fusion.4
  71.1 1.0 copy.75
  72.1 5.7 %all-to-all-done.2 = bf16[16,64,128]{2,1,0:T(8,128)(2,1)S(1)} async-done(((bf16[16,64,128]{2,1,0:T(8,128)(2,1)}), bf16[16,64,128]{2,1,0:T(8,128)(2,1)S(1)}, u32[]{:S(2)}, u32[]{:S(2)}) %all-to-all-start.2) | async-done | bytes 262176 | tf_op jit(solution)/shard_map/all_to_all | solution.py:70
  77.8 5.6 %all-to-all-start = ((bf16[16,64,256]{2,1,0:T(8,128)(2,1)}), bf16[16,64,256]{2,1,0:T(8,128)(2,1)S(1)}, u32[]{:S(2)}, u32[]{:S(2)}) async-start(bf16[16,64,256]{2,1,0:T(8,128)(2,1)} %copy.75), calls=%async_computation | async-start | bytes 1048576 | tf_op jit(solution)/shard_map/all_to_all | solution.py:62
  83.4 0.0 copy-done.1
  83.4 0.2 convolution_bitcast_fusion.10
  83.7 0.3 fusion.49
  84.0 0.2 convolution_bitcast_fusion.5
  84.2 0.2 convolution_bitcast_fusion.4
  84.4 0.8 pad_maximum_fusion.2
  85.2 2.0 copy.86
  87.3 9.8 %all-to-all-done = bf16[16,64,256]{2,1,0:T(8,128)(2,1)S(1)} async-done(((bf16[16,64,256]{2,1,0:T(8,128)(2,1)}), bf16[16,64,256]{2,1,0:T(8,128)(2,1)S(1)}, u32[]{:S(2)}, u32[]{:S(2)}) %all-to-all-start) | async-done | bytes 524320 | tf_op jit(solution)/shard_map/all_to_all | solution.py:62
  97.0 4.8 %all-to-all-start.5 = ((f32[16,64,128]{2,1,0:T(8,128)}), f32[16,64,128]{2,1,0:T(8,128)}, u32[]{:S(2)}, u32[]{:S(2)}) async-start(f32[16,64,128]{2,1,0:T(8,128)} %bitcast.98), calls=%async_computation.5 | async-start | bytes 1048576 | tf_op jit(solution)/shard_map/all_to_all | solution.py:94
  101.9 0.3 convolution_bitcast_fusion.8
  102.1 0.3 fusion.36
  102.4 13.1 %all-to-all-done.5 = f32[16,64,128]{2,1,0:T(8,128)} async-done(((f32[16,64,128]{2,1,0:T(8,128)}), f32[16,64,128]{2,1,0:T(8,128)}, u32[]{:S(2)}, u32[]{:S(2)}) %all-to-all-start.5) | async-done | bytes 524320 | tf_op jit(solution)/shard_map/all_to_all | solution.py:94
  115.6 1.3 copy.87
  116.9 1.1 broadcast_multiply_fusion
  118.1 3.6 %all-to-all-start.6 = ((f32[2,16,64,128]{3,1,2,0:T(8,128)}), f32[2,16,64,128]{3,1,2,0:T(8,128)S(1)}, u32[]{:S(2)}, u32[]{:S(2)}) async-start(f32[2,16,64,128]{3,1,2,0:T(8,128)} %broadcast_multiply_fusion), calls=%async_computation.6 | async-start | bytes 2097152 | tf_op jit(solution)/shard_map/all_to_all | solution.py:106
  121.7 0.2 convolution_bitcast_fusion.3
  121.9 1.2 convolution_bitcast_fusion.2
  123.0 1.0 pad_maximum_fusion.1
  124.1 2.5 copy.84
  126.6 8.6 %all-to-all-done.6 = f32[2,16,64,128]{3,1,2,0:T(8,128)S(1)} async-done(((f32[2,16,64,128]{3,1,2,0:T(8,128)}), f32[2,16,64,128]{3,1,2,0:T(8,128)S(1)}, u32[]{:S(2)}, u32[]{:S(2)}) %all-to-all-start.6) | async-done | bytes 1048608 | tf_op jit(solution)/shard_map/all_to_all | solution.py:106
  135.2 5.7 %all-to-all-start.4 = ((f32[16,64,256]{2,1,0:T(8,128)}), f32[16,64,256]{2,1,0:T(8,128)}, u32[]{:S(2)}, u32[]{:S(2)}) async-start(f32[16,64,256]{2,1,0:T(8,128)} %bitcast.90), calls=%async_computation.4 | async-start | bytes 2097152 | tf_op jit(solution)/shard_map/all_to_all | solution.py:83
  141.0 0.0 all-gather.3.cloned.1.call-done
  141.0 0.0 copy-start.5
  141.0 1.3 dynamic-slice_bitcast_fusion
  142.4 0.3 convolution_bitcast_fusion.6
  142.7 0.4 fusion.27
  143.1 0.3 convolution_bitcast_fusion.1
  143.4 0.3 convolution_bitcast_fusion
  143.7 1.5 pad_maximum_fusion
  145.2 2.9 copy.82
  148.1 17.8 %all-to-all-done.4 = f32[16,64,256]{2,1,0:T(8,128)} async-done(((f32[16,64,256]{2,1,0:T(8,128)}), f32[16,64,256]{2,1,0:T(8,128)}, u32[]{:S(2)}, u32[]{:S(2)}) %all-to-all-start.4) | async-done | bytes 1048608 | tf_op jit(solution)/shard_map/all_to_all | solution.py:83
  165.8 4.8 %all-to-all-start.3 = ((f32[16,64,512]{2,1,0:T(8,128)}), f32[16,64,512]{2,1,0:T(8,128)}, u32[]{:S(2)}, u32[]{:S(2)}) async-start(f32[16,64,512]{2,1,0:T(8,128)} %bitcast.89), calls=%async_computation.3 | async-start | bytes 4194304 | tf_op jit(solution)/shard_map/all_to_all | solution.py:76
  170.7 0.1 copy.88
  170.8 0.6 convolution_convert_fusion
  171.4 1.0 copy.91
  172.5 5.4 %fusion.8 = f32[64,64,256]{2,0,1:T(8,128)} fusion(f32[16,64,256]{2,1,0:T(8,128)} %all-to-all-done.4, s32[16]{0:T(128)S(1)} %get-tuple-element.27), kind=kOutput, calls=%fused_computation.24 | convolution fusion | flops 201327616 | bytes 5242944 | tf_op jit(solution)/shard_map/mk,mrh->krh/dot_general | solution.py:43
  177.8 0.3 fusion.12
  178.2 0.2 convolution_add_fusion.1
  178.4 0.4 copy-done.7
  178.8 1.0 fusion.7
  179.7 38.5 %all-to-all-done.3 = f32[16,64,512]{2,1,0:T(8,128)} async-done(((f32[16,64,512]{2,1,0:T(8,128)}), f32[16,64,512]{2,1,0:T(8,128)}, u32[]{:S(2)}, u32[]{:S(2)}) %all-to-all-start.3) | async-done | bytes 2097184 | tf_op jit(solution)/shard_map/all_to_all | solution.py:76
  218.2 3.5 %fusion = f32[4,64,512]{2,0,1:T(4,128)S(1)} fusion(f32[16,64,512]{2,1,0:T(8,128)} %all-to-all-done.3, s32[16]{0:T(128)S(1)} %get-tuple-element.26), kind=kOutput, calls=%fused_computation.1 | convolution fusion | flops 25165888 | bytes 2621504 | tf_op jit(solution)/shard_map/mk,mrh->krh/dot_general | solution.py:43
  221.7 111.2 %all-reduce.2 = (bf16[4,64,512]{2,0,1:T(4,128)(2,1)S(1)}, bf16[64,64,256]{2,0,1:T(8,128)(2,1)}) all-reduce(f32[4,64,512]{2,0,1:T(4,128)S(1)} %fusion, f32[64,64,256]{2,0,1:T(8,128)} %fusion.8), channel_id=1, replica_groups=mesh['grp'=2,'mem'=16] {'grp'}, use_global_device_ids=true, to_apply=%region_1.2 | all-reduce | flops 1179648 | bytes 7077888 | tf_op jit(solution)/shard_map/psum | solution.py:93
  332.8 0.7 copy.89
  333.6 4.1 %copy.90 = bf16[64,64,256]{2,1,0:T(8,128)(2,1)} copy(bf16[64,64,256]{2,0,1:T(8,128)(2,1)} %get-tuple-element.25) | data formatting | bytes 4194304
  (21 shorter events, 0.1 us)
Async XLA Ops:
  7.2 62.7 %copy-start = (bf16[64,64,256]{2,1,0:T(8,128)(2,1)S(1)}, bf16[64,64,256]{2,1,0:T(8,128)(2,1)}, u32[]{:S(2)}) copy-start(bf16[64,64,256]{2,1,0:T(8,128)(2,1)} %param.10) | copy-start | bytes 6291460
  7.2 133.8 %all-gather.3.cloned.1.call-start = ((), (), s32[]{:S(2)}) async-start(), calls=%async_computation.7 | async-start | bytes 4456448 | tf_op jit(solution)/shard_map/all_gather | solution.py:60
  44.5 11.5 %all-to-all-start.1 = ((bf16[2,16,64,128]{3,1,2,0:T(8,128)(2,1)}), bf16[2,16,64,128]{3,1,2,0:T(8,128)(2,1)S(1)}, u32[]{:S(2)}, u32[]{:S(2)}) async-start(bf16[2,16,64,128]{3,1,2,0:T(8,128)(2,1)} %copy.79), calls=%async_computation.1 | async-start | bytes 1048576 | tf_op jit(solution)/shard_map/all_to_all | solution.py:68
  57.0 20.9 %all-to-all-start.2 = ((bf16[16,64,128]{2,1,0:T(8,128)(2,1)}), bf16[16,64,128]{2,1,0:T(8,128)(2,1)S(1)}, u32[]{:S(2)}, u32[]{:S(2)}) async-start(bf16[16,64,128]{2,1,0:T(8,128)(2,1)} %copy.81), calls=%async_computation.2 | async-start | bytes 524288 | tf_op jit(solution)/shard_map/all_to_all | solution.py:70
  69.9 13.5 %copy-start.1 = (bf16[128,1024]{1,0:T(8,128)(2,1)S(1)}, bf16[128,1024]{1,0:T(8,128)(2,1)}, u32[]{:S(2)}) copy-start(bf16[128,1024]{1,0:T(8,128)(2,1)} %param.6) | copy-start | bytes 786436
  69.9 13.8 %copy-start.4 = (bf16[128,1024]{1,0:T(8,128)(2,1)S(1)}, bf16[128,1024]{1,0:T(8,128)(2,1)}, u32[]{:S(2)}) copy-start(bf16[128,1024]{1,0:T(8,128)(2,1)} %param.7) | copy-start | bytes 786436
  77.8 7.4 %copy-start.6 = (bf16[16,64,128]{2,1,0:T(8,128)(2,1)}, bf16[16,64,128]{2,1,0:T(8,128)(2,1)S(1)}, u32[]{:S(2)}) copy-start(bf16[16,64,128]{2,1,0:T(8,128)(2,1)S(1)} %all-to-all-done.2) | copy-start | bytes 786436
  77.8 19.2 %all-to-all-start = ((bf16[16,64,256]{2,1,0:T(8,128)(2,1)}), bf16[16,64,256]{2,1,0:T(8,128)(2,1)S(1)}, u32[]{:S(2)}, u32[]{:S(2)}) async-start(bf16[16,64,256]{2,1,0:T(8,128)(2,1)} %copy.75), calls=%async_computation | async-start | bytes 1048576 | tf_op jit(solution)/shard_map/all_to_all | solution.py:62
  97.0 21.0 %copy-start.8 = (bf16[16,64,256]{2,1,0:T(8,128)(2,1)}, bf16[16,64,256]{2,1,0:T(8,128)(2,1)S(1)}, u32[]{:S(2)}) copy-start(bf16[16,64,256]{2,1,0:T(8,128)(2,1)S(1)} %all-to-all-done) | copy-start | bytes 1572868
  97.0 18.5 %all-to-all-start.5 = ((f32[16,64,128]{2,1,0:T(8,128)}), f32[16,64,128]{2,1,0:T(8,128)}, u32[]{:S(2)}, u32[]{:S(2)}) async-start(f32[16,64,128]{2,1,0:T(8,128)} %bitcast.98), calls=%async_computation.5 | async-start | bytes 1048576 | tf_op jit(solution)/shard_map/all_to_all | solution.py:94
  118.1 17.1 %all-to-all-start.6 = ((f32[2,16,64,128]{3,1,2,0:T(8,128)}), f32[2,16,64,128]{3,1,2,0:T(8,128)S(1)}, u32[]{:S(2)}, u32[]{:S(2)}) async-start(f32[2,16,64,128]{3,1,2,0:T(8,128)} %broadcast_multiply_fusion), calls=%async_computation.6 | async-start | bytes 2097152 | tf_op jit(solution)/shard_map/all_to_all | solution.py:106
  124.1 16.8 %copy-start.10 = (s32[1,3]{1,0:T(1,128)S(1)}, s32[1,3]{1,0:T(1,128)}, u32[]{:S(2)}) copy-start(s32[1,3]{1,0:T(1,128)} %param.8) | copy-start | bytes 40
  135.2 30.6 %all-to-all-start.4 = ((f32[16,64,256]{2,1,0:T(8,128)}), f32[16,64,256]{2,1,0:T(8,128)}, u32[]{:S(2)}, u32[]{:S(2)}) async-start(f32[16,64,256]{2,1,0:T(8,128)} %bitcast.90), calls=%async_computation.4 | async-start | bytes 2097152 | tf_op jit(solution)/shard_map/all_to_all | solution.py:83
  141.0 1.7 copy-start.5
  142.4 1.0 copy-start.2
  165.8 52.4 %all-to-all-start.3 = ((f32[16,64,512]{2,1,0:T(8,128)}), f32[16,64,512]{2,1,0:T(8,128)}, u32[]{:S(2)}, u32[]{:S(2)}) async-start(f32[16,64,512]{2,1,0:T(8,128)} %bitcast.89), calls=%async_computation.3 | async-start | bytes 4194304 | tf_op jit(solution)/shard_map/all_to_all | solution.py:76
  172.4 5.4 %copy-start.3 = (bf16[1024,512]{1,0:T(8,128)(2,1)S(1)}, bf16[1024,512]{1,0:T(8,128)(2,1)}, u32[]{:S(2)}) copy-start(bf16[1024,512]{1,0:T(8,128)(2,1)} %copy-done.2) | copy-start | bytes 3145732
  172.4 5.7 %copy-start.9 = (bf16[16,64,256]{2,1,0:T(8,128)(2,1)S(1)}, bf16[16,64,256]{2,1,0:T(8,128)(2,1)}, u32[]{:S(2)}) copy-start(bf16[16,64,256]{2,1,0:T(8,128)(2,1)} %copy-done.8) | copy-start | bytes 1572868
  177.8 1.0 copy-start.7
Sparse Core Ops, SparseCore 0:
  10.2 51.1 all-gather.2
where the time goes:
time: 347 us; the launch traced here: 344 us
  blocking collectives  145 us (42%)
  waiting for transfers between devices  102 us (29%)
  starting transfers between devices  40.9 us (12%)
  local copies, waits for them, and re-layouts  19.3 us (6%)
  matrix products  17.8 us (5%)
  between operations  14.4 us (4%)
  other arithmetic  4.69 us (1%)
    psum x1, blocking collectives, on_device(): coarse_total, middle_total = lax.psum((coarse_local, middle_local), 'grp')  111 us
    all_to_all x1, waiting for transfers between devices, on_device(): lax.all_to_all(coarse_term.reshape(member_count, row_count, -1), 'mem', s...  38.5 us
    all_gather x1, blocking collectives, on_device(): all_paths = lax.all_gather(path, ('grp', 'mem'), axis=0, tiled=True)  34.2 us
    all_to_all x1, waiting for transfers between devices, on_device(): lax.all_to_all(middle_term.reshape(member_count, row_count, -1), 'mem', s...  17.8 us
    all_to_all x1, waiting for transfers between devices, on_device(): lax.all_to_all(fine_term.reshape(member_count, row_count, -1), 'mem', spl...  13.1 us
    all_to_all x1, starting transfers between devices, on_device(): lax.all_to_all(merged, 'mem', split_axis=0, concat_axis=1, tiled=True)[0]  12.9 us
    all_to_all x1, waiting for transfers between devices, on_device(): lax.all_to_all(middle_send, 'mem', split_axis=0, concat_axis=1, tiled=True)  9.76 us
    dot_general x3, matrix products, collect_blocks(): jnp.einsum('mk,mrh->krh', picker.astype(jnp.float32), pieces, precision=l...  9.46 us
  transfers between devices with their start and end apart: 8, of which 7 were waited for; matrix products, arithmetic and copies ran while one was open for 10% of the time, Pallas kernels for 0%

commit v1 on v0

v1 whole, which is shorter than its diff:
```python
import functools
import math

import jax
import jax.numpy as jnp
from jax import lax
from jax.experimental import pallas as pl
from jax.experimental.pallas import tpu as pltpu
from jax.sharding import PartitionSpec as P

MESH = pl.DeviceIdType.MESH
LANES = 128
F32 = jnp.float32
BF16 = jnp.bfloat16


def path_kernel(groups, members, row_ref, all_ref, send_sem, recv_sem):
    group = lax.axis_index("grp")
    member = lax.axis_index("mem")
    count = groups * members
    me = group * members + member
    barrier = pltpu.get_barrier_semaphore()

    def place(step):
        other = lax.rem(me + step, count)
        return other, (other // members, lax.rem(other, members))

    def greet(step, carry):
        _, where = place(step)
        pl.semaphore_signal(barrier, inc=1, device_id=where, device_id_type=MESH)
        return carry

    lax.fori_loop(1, count, greet, 0)
    pl.semaphore_wait(barrier, count - 1)

    def copy(step):
        other, where = place(step)
        return other, where

    def send(step, carry):
        other, where = place(step)
        pltpu.make_async_remote_copy(
            src_ref=row_ref.at[0],
            dst_ref=all_ref.at[me],
            send_sem=send_sem.at[other],
            recv_sem=recv_sem.at[me],
            device_id=where,
            device_id_type=MESH,
        ).start()
        return carry

    lax.fori_loop(1, count, send, 0)
    all_ref[me] = row_ref[0]

    def finish(step, carry):
        other, where = place(step)
        done = pltpu.make_async_remote_copy(
            src_ref=row_ref.at[0],
            dst_ref=all_ref.at[other],
            send_sem=send_sem.at[other],
            recv_sem=recv_sem.at[other],
            device_id=where,
            device_id_type=MESH,
        )
        done.wait_send()
        done.wait_recv()
        return carry

    lax.fori_loop(1, count, finish, 0)


def gather_paths(path, groups, members):
    count = groups * members
    row = jnp.pad(path, ((0, 0), (0, LANES - path.shape[1])))[:, None, :]
    out = pl.pallas_call(
        functools.partial(path_kernel, groups, members),
        out_shape=jax.ShapeDtypeStruct((count, 1, LANES), jnp.int32),
        in_specs=[pl.BlockSpec(memory_space=pltpu.VMEM)],
        out_specs=pl.BlockSpec(memory_space=pltpu.VMEM),
        scratch_shapes=[
            pltpu.SemaphoreType.DMA((count,)),
            pltpu.SemaphoreType.DMA((count,)),
        ],
        compiler_params=pltpu.CompilerParams(collective_id=0, has_side_effects=True),
        name="path_gather",
    )(row)
    return out[:, 0, : path.shape[1]].reshape(-1)


def gelu_parts(before, hidden_grad):
    scale = math.sqrt(2.0 / math.pi)
    square = before * before
    tanh = jnp.tanh(scale * (before + 0.044715 * (square * before)))
    half = 0.5 * (1.0 + tanh)
    hidden = before * half
    slope = half + 0.5 * before * (1.0 - tanh * tanh) * (scale * (1.0 + 3 * 0.044715 * square))
    return hidden.astype(BF16), (hidden_grad * slope).astype(BF16)


def dot(left, right):
    return jnp.dot(left, right, preferred_element_type=F32)


def dot_transposed(left, right):
    return lax.dot_general(left, right, (((1,), (1,)), ((), ())), preferred_element_type=F32)


def level(weights, x, g, xt, gt):
    width = weights.shape[1]
    half = width // 2
    if half % LANES == 0:
        up = weights[:, :half]
        down = weights[:, half:]
        hidden, grad = gelu_parts(dot(x, up), dot(g, down))
        term = jnp.concatenate(
            [dot(xt, grad).astype(BF16), dot(gt, hidden).astype(BF16)], axis=1
        )
        return term, dot_transposed(grad, up)
    before = dot(x, weights)
    hidden_grad = pltpu.roll(dot(g, weights), half, 1)
    hidden, grad = gelu_parts(before, hidden_grad)
    first = lax.broadcasted_iota(jnp.int32, grad.shape, 1) < half
    grad = jnp.where(first, grad.astype(F32), 0.0).astype(BF16)
    hidden = jnp.where(first, hidden.astype(F32), 0.0)
    hidden = pltpu.roll(hidden, half, 1).astype(BF16)
    term = (dot(xt, grad) + dot(gt, hidden)).astype(BF16)
    return term, dot_transposed(grad, weights)


def main_kernel(
    groups,
    members,
    path,
    tokens,
    cotangent,
    coarse_w,
    middle_w,
    fine_w,
    tokens_grad,
    middle_parts,
    fine_parts,
    coarse_own,
    coarse_others,
    coarse_send,
    middle_send,
    fine_out,
    fine_in,
    fine_send,
    coarse_block,
    middle_block,
    fine_block,
    coarse_term,
    middle_term,
    fine_term,
    coarse_parts,
    coarse_half,
    xt,
    gt,
    total,
    mem_send,
    mem_recv,
    grp_send,
    grp_recv,
):
    group = lax.axis_index("grp")
    me = lax.axis_index("mem")
    owned = fine_w.shape[0]

    barrier = pltpu.get_barrier_semaphore()

    def greet_member(step, carry):
        pl.semaphore_signal(
            barrier,
            inc=1,
            device_id={"mem": lax.rem(me + step, members)},
            device_id_type=MESH,
        )
        return carry

    def greet_group(step, carry):
        pl.semaphore_signal(
            barrier,
            inc=1,
            device_id={"grp": lax.rem(group + step, groups)},
            device_id_type=MESH,
        )
        return carry

    lax.fori_loop(1, members, greet_member, 0)
    lax.fori_loop(1, groups, greet_group, 0)

    def route(document, column):
        return path[document * 3 + column]

    def pick_fine(index, carry):
        identity = route(index, 2)
        place = jnp.clip(identity - group * owned, 0, owned - 1)
        fine_out[index // members, lax.rem(index, members)] = fine_w[place]
        return carry

    lax.fori_loop(0, groups * members, pick_fine, 0)

    def pick_middle(p, carry):
        middle_send[p] = middle_w[route(group * members + p, 1)]
        return carry

    def pick_coarse(p, carry):
        coarse_send[p] = coarse_w[route(group * members + p, 0)]
        return carry

    lax.fori_loop(0, members, pick_middle, 0)

    pl.semaphore_wait(barrier, members - 1 + groups - 1)

    def member_copy(slot, source, target, out_slot, in_slot, p):
        return pltpu.make_async_remote_copy(
            src_ref=source.at[out_slot],
            dst_ref=target.at[in_slot],
            send_sem=mem_send.at[slot, p],
            recv_sem=mem_recv.at[slot, in_slot],
            device_id={"mem": p},
            device_id_type=MESH,
        )

    def spread(slot, source, target):
        def body(step, carry):
            p = lax.rem(me + step, members)
            member_copy(slot, source, target, p, me, p).start()
            return carry

        lax.fori_loop(1, members, body, 0)

    def arrive(slot, source, target):
        def body(step, carry):
            p = lax.rem(me + members - step, members)
            member_copy(slot, source, target, p, p, p).wait_recv()
            return carry

        lax.fori_loop(1, members, body, 0)

    def left(slot, source, target):
        def body(step, carry):
            p = lax.rem(me + step, members)
            member_copy(slot, source, target, p, p, p).wait_send()
            return carry

        lax.fori_loop(1, members, body, 0)

    def group_copy(slot, source, target, in_slot, other):
        return pltpu.make_async_remote_copy(
            src_ref=source,
            dst_ref=target.at[in_slot],
            send_sem=grp_send.at[slot, other],
            recv_sem=grp_recv.at[slot, in_slot],
            device_id={"grp": other},
            device_id_type=MESH,
        )

    def group_spread(slot, source_of, target):
        def body(step, carry):
            other = lax.rem(group + step, groups)
            group_copy(slot, source_of(other), target, group, other).start()
            return carry

        lax.fori_loop(1, groups, body, 0)

    def group_arrive(slot, source_of, target):
        def body(step, carry):
            other = lax.rem(group + step, groups)
            group_copy(slot, source_of(other), target, other, other).wait_recv()
            return carry

        lax.fori_loop(1, groups, body, 0)

    def group_left(slot, source_of, target):
        def body(step, carry):
            other = lax.rem(group + step, groups)
            group_copy(slot, source_of(other), target, other, other).wait_send()
            return carry

        lax.fori_loop(1, groups, body, 0)

    fine_source = lambda other: fine_out.at[other]
    group_spread(0, fine_source, fine_in)
    spread(0, middle_send, middle_block)
    middle_block[me] = middle_send[me]
    lax.fori_loop(0, members, pick_coarse, 0)
    coarse_block[me] = coarse_send[me]
    fine_in[group] = fine_out[group]
    group_arrive(0, fine_source, fine_in)

    def merge_fine(p, carry):
        owner = route(group * members + p, 2) // owned
        fine_send[p] = fine_in[owner, p]
        return carry

    lax.fori_loop(0, members, merge_fine, 0)
    spread(1, fine_send, fine_block)
    spread(2, coarse_send, coarse_block)
    fine_block[me] = fine_send[me]

    width = tokens.shape[1]
    for start in range(0, width, LANES):
        columns = slice(start, start + LANES)
        xt[columns, :] = tokens[:, columns].T
        gt[columns, :] = cotangent[:, columns].T

    def compute(block, term):
        weights = block[...].reshape(width, block.shape[2])
        value, part = level(weights, tokens[...], cotangent[...], xt[...], gt[...])
        term[...] = value.reshape(term.shape)
        return part

    middle_own = middle_parts.at[group]
    fine_own = fine_parts.at[group]

    arrive(0, middle_send, middle_block)
    total[...] = compute(middle_block, middle_term)
    spread(3, middle_term, middle_own)
    middle_parts[group, me] = middle_term[me]

    arrive(1, fine_send, fine_block)
    total[...] += compute(fine_block, fine_term)
    spread(4, fine_term, fine_own)
    fine_parts[group, me] = fine_term[me]

    arrive(2, coarse_send, coarse_block)
    part = compute(coarse_block, coarse_term)
    spread(5, coarse_term, coarse_parts)
    coarse_parts[me] = coarse_term[me]
    tokens_grad[...] = (total[...] + part).astype(BF16)

    arrive(3, middle_term, middle_own)
    middle_source = lambda other: middle_own
    group_spread(1, middle_source, middle_parts)
    arrive(4, fine_term, fine_own)
    fine_own_source = lambda other: fine_own
    group_spread(2, fine_own_source, fine_parts)

    left(0, middle_send, middle_block)
    left(1, fine_send, fine_block)
    left(2, coarse_send, coarse_block)
    group_left(0, fine_source, fine_in)
    left(3, middle_term, middle_own)
    left(4, fine_term, fine_own)

    coarse_own[...] = jnp.zeros_like(coarse_own)
    coarse_others[group] = jnp.zeros(coarse_others.shape[1:], BF16)
    arrive(5, coarse_term, coarse_parts)

    def add_coarse(p, carry):
        identity = route(group * members + p, 0)
        piece = coarse_parts[p].astype(F32)
        for k in range(coarse_own.shape[0]):
            coarse_own[k] += piece * jnp.where(identity == k, 1.0, 0.0)
        return carry

    lax.fori_loop(0, members, add_coarse, 0)
    coarse_half[...] = coarse_own[...].astype(BF16)
    coarse_source = lambda other: coarse_half
    group_spread(3, coarse_source, coarse_others)
    left(5, coarse_term, coarse_parts)
    group_arrive(1, middle_source, middle_parts)
    group_arrive(2, fine_own_source, fine_parts)
    group_arrive(3, coarse_source, coarse_others)
    group_left(1, middle_source, middle_parts)
    group_left(2, fine_own_source, fine_parts)
    group_left(3, coarse_source, coarse_others)


def exchange(paths, tokens, cotangent, coarse_w, middle_w, fine_w, groups, members):
    rows = coarse_w.shape[1]
    wide, medium, narrow = coarse_w.shape[2], middle_w.shape[2], fine_w.shape[2]
    token_count, width = tokens.shape

    def stack(size, kind=BF16):
        return pltpu.VMEM((members, rows, size), kind)

    vmem = pl.BlockSpec(memory_space=pltpu.VMEM)
    return pl.pallas_call(
        functools.partial(main_kernel, groups, members),
        out_shape=(
            jax.ShapeDtypeStruct(tokens.shape, BF16),
            jax.ShapeDtypeStruct((groups, members, rows, medium), BF16),
            jax.ShapeDtypeStruct((groups, members, rows, narrow), BF16),
            jax.ShapeDtypeStruct(coarse_w.shape, F32),
            jax.ShapeDtypeStruct((groups,) + coarse_w.shape, BF16),
        ),
        in_specs=[pl.BlockSpec(memory_space=pltpu.SMEM)] + [vmem] * 5,
        out_specs=(vmem,) * 5,
        scratch_shapes=[
            stack(wide),
            stack(medium),
            pltpu.VMEM((groups, members, rows, narrow), BF16),
            pltpu.VMEM((groups, members, rows, narrow), BF16),
            stack(narrow),
            stack(wide),
            stack(medium),
            stack(narrow),
            stack(wide),
            stack(medium),
            stack(narrow),
            stack(wide),
            pltpu.VMEM(coarse_w.shape, BF16),
            pltpu.VMEM((width, token_count), BF16),
            pltpu.VMEM((width, token_count), BF16),
            pltpu.VMEM((token_count, width), F32),
            pltpu.SemaphoreType.DMA((6, members)),
            pltpu.SemaphoreType.DMA((6, members)),
            pltpu.SemaphoreType.DMA((4, groups)),
            pltpu.SemaphoreType.DMA((4, groups)),
        ],
        compiler_params=pltpu.CompilerParams(
            collective_id=1, has_side_effects=True, vmem_limit_bytes=60 * 2**20
        ),
        name="exchange",
    )(paths, tokens, cotangent, coarse_w, middle_w, fine_w)


def collect_kernel(
    path,
    first_owned,
    middle_parts,
    fine_parts,
    coarse_own,
    coarse_others,
    coarse_grad,
    middle_grad,
    fine_grad,
    middle_sum,
    fine_sum,
):
    owned = fine_grad.shape[0]
    middle_sum[...] = jnp.zeros_like(middle_sum)
    fine_sum[...] = jnp.zeros_like(fine_sum)

    def add(document, carry):
        k = path[document * 3 + 1]
        middle_sum[k] += middle_parts[document].astype(F32)
        place = path[document * 3 + 2] - first_owned[0]

        @pl.when((place >= 0) & (place < owned))
        def _():
            fine_sum[place] += fine_parts[document].astype(F32)

        return carry

    lax.fori_loop(0, middle_parts.shape[0], add, 0)
    middle_grad[...] = middle_sum[...].astype(BF16)
    fine_grad[...] = fine_sum[...].astype(BF16)
    coarse = coarse_own[...]
    for other in range(coarse_others.shape[0]):
        coarse = coarse + coarse_others[other].astype(F32)
    coarse_grad[...] = coarse.astype(BF16)


def collect(paths, first_owned, middle_parts, fine_parts, coarse_own, coarse_others, shapes):
    vmem = pl.BlockSpec(memory_space=pltpu.VMEM)
    smem = pl.BlockSpec(memory_space=pltpu.SMEM)
    return pl.pallas_call(
        collect_kernel,
        out_shape=tuple(jax.ShapeDtypeStruct(shape, BF16) for shape in shapes),
        in_specs=[smem, smem] + [vmem] * 4,
        out_specs=(vmem,) * 3,
        scratch_shapes=[pltpu.VMEM(shapes[1], F32), pltpu.VMEM(shapes[2], F32)],
        compiler_params=pltpu.CompilerParams(vmem_limit_bytes=60 * 2**20),
        name="collect",
    )(paths, first_owned, middle_parts, fine_parts, coarse_own, coarse_others)


def on_device(tokens, cotangent, path, coarse_weights, middle_weights, fine_weights):
    members = lax.axis_size("mem")
    groups = lax.axis_size("grp")
    paths = gather_paths(path, groups, members)
    tokens_grad, middle_parts, fine_parts, coarse_own, coarse_others = exchange(
        paths, tokens, cotangent, coarse_weights, middle_weights, fine_weights, groups, members
    )
    first_owned = (lax.axis_index("grp") * fine_weights.shape[0]).astype(jnp.int32).reshape(1)
    flat = lambda parts: parts.reshape((groups * members,) + parts.shape[2:])
    grads = collect(
        paths,
        first_owned,
        flat(middle_parts),
        flat(fine_parts),
        coarse_own,
        coarse_others,
        (coarse_weights.shape, middle_weights.shape, fine_weights.shape),
    )
    return (tokens_grad,) + tuple(grads)


def solution(mesh):
    return jax.shard_map(
        on_device,
        mesh=mesh,
        in_specs=(
            P(("grp", "mem"), None),
            P(("grp", "mem"), None),
            P(("grp", "mem"), None),
            P(None, "mem", None),
            P(None, "mem", None),
            P("grp", "mem", None),
        ),
        out_specs=(
            P(("grp", "mem"), None),
            P(None, "mem", None),
            P(None, "mem", None),
            P("grp", "mem", None),
        ),
        check_vma=False,
    )
```

time: 347 us -> 120 us (0.35)
  blocking collectives: 145 us -> 0 us
  Pallas kernels: 0 us -> 115 us
  waiting for transfers between devices: 102 us -> 0 us
  starting transfers between devices: 40.9 us -> 0 us
  matrix products: 17.8 us -> 0 us
  local copies, waits for them, and re-layouts: 19.3 us -> 3.25 us
  between operations: 14.4 us -> 0.66 us
  other arithmetic: 4.69 us -> 0 us
    pallas_call x0 -> x3, Pallas kernels: none -> 115 us  [the longest x1 101 us: exchange(): pl.pallas_call(functools.partial(main_kernel, groups, members), out_shape...]
    psum x1 -> x0, blocking collectives: 111 us -> none  [on_device(): coarse_total, middle_total = lax.psum((coarse_local, middle_local), 'grp')]
    all_to_all x7 -> x0, waiting for transfers between devices: 101 us -> none  [the longest x1 38.5 us: on_device(): lax.all_to_all(coarse_term.reshape(member_count, row_count, -1), 'mem', s...]
    all_to_all x7 -> x0, starting transfers between devices: 40.9 us -> none  [the longest x1 12.9 us: on_device(): lax.all_to_all(merged, 'mem', split_axis=0, concat_axis=1, tiled=True)[0]]
    all_gather x1 -> x0, blocking collectives: 34.2 us -> none  [on_device(): all_paths = lax.all_gather(path, ('grp', 'mem'), axis=0, tiled=True)]
    dot_general x20 -> x0, matrix products: 17.8 us -> none  [the longest x3 9.46 us: collect_blocks(): jnp.einsum('mk,mrh->krh', picker.astype(jnp.float32), pieces, precision=l...]
    concatenate x3 -> x0, local copies, waits for them, and re-layouts: 7.48 us -> none  [level_terms(): return (jnp.concatenate([up_grad, down_grad], axis=1), input_part)]
    unnamed x25 -> x3, local copies, waits for them, and re-layouts: 6.26 us -> 0.71 us
  transfers between devices with their start and end apart: 8 -> 0, of which waited for: 7 -> 0; matrix products, arithmetic and copies ran while one was open for 10% -> 0% of each run, Pallas kernels for 0% -> 0%
where the time goes in v1:
time: 120 us; the launch traced here: 119 us
  Pallas kernels  115 us (96%)
  local copies, waits for them, and re-layouts  3.25 us (3%)
    pallas_call x1, Pallas kernels, exchange(): pl.pallas_call(functools.partial(main_kernel, groups, members), out_shape...  101 us
    pallas_call x1, Pallas kernels, gather_paths(): pl.pallas_call(functools.partial(path_kernel, groups, members), out_shape...  9.55 us
    pallas_call x1, Pallas kernels, collect(): pl.pallas_call(collect_kernel, out_shape=tuple((jax.ShapeDtypeStruct(shap...  4.46 us

profile of v1, /device:TPU:11, one launch (start us, length us, event | category | flops | bytes accessed | tf_op | source)
XLA Modules:
  0.0 119.3 jit_solution(17033201552551843521)
XLA Ops:
  0.6 1.2 pad_bitcast_fusion.row_ref
  1.8 9.5 %path_gather.1 = s32[32,1,128]{2,1,0:T(1,128)} custom-call(s32[1,1,128]{2,1,0:T(1,128)} %pad_bitcast_fusion.row_ref), custom_call_target="tpu_custom_call" | custom-call | tf_op jit(solution)/shard_map/path_gather/pallas_call | solution.py:75
  11.4 0.8 slice_reduce_fusion
  12.1 0.6 reshape_squeeze.3.path
  12.7 101.4 %exchange.1 = (bf16[128,1024]{1,0:T(8,128)(2,1)}, bf16[2,16,64,256]{3,2,1,0:T(8,128)(2,1)}, bf16[2,16,64,128]{3,2,1,0:T(8,128)(2,1)}, f32[4,64,512]{2,1,0:T(8,128)}, bf16[2,4,64,512]{3,2,1,0:T(8,128)(2,1)}) custom-call(s32[96]{0:T(128)} %reshape_squeeze.3.path, bf16[128,1024]{1,0:T(8,128)(2,1)} %tokens.1, bf16[128,1024]{1,0:T(8,128)(2,1)} %cotangent.1, ...), custom_call_target="tpu_custom_call" | custom-call | tf_op jit(solution)/shard_map/exchange/pallas_call | solution.py:380
  114.1 0.0 copy-start
  114.1 4.5 %collect.1 = (bf16[4,64,512]{2,1,0:T(8,128)(2,1)}, bf16[64,64,256]{2,1,0:T(8,128)(2,1)}, bf16[32,64,128]{2,1,0:T(8,128)(2,1)}) custom-call(s32[96]{0:T(128)} %reshape_squeeze.3.path, s32[1]{0:T(128)} %bitcast.1.first_owned, bf16[32,64,256]{2,1,0:T(8,128)(2,1)} %bitcast.5, bf16[32,64,128]{2,1,0:T(8,128)(2,1)} %bitcast.6, ...), custom_call_target="tpu_custom_call" | custom-call | tf_op jit(solution)/shard_map/collect/pallas_call | solution.py:460
  118.6 0.0 copy-done
  118.6 0.7 copy.11
Async XLA Ops:
  114.1 4.5 %copy-start = (bf16[128,1024]{1,0:T(8,128)(2,1)S(1)}, bf16[128,1024]{1,0:T(8,128)(2,1)}, u32[]{:S(2)}) copy-start(bf16[128,1024]{1,0:T(8,128)(2,1)} %get-tuple-element.24) | copy-start | bytes 786436

commit v2 on v1

v2 whole, which is shorter than its diff:
```python
import functools
import math

import jax
import jax.numpy as jnp
from jax import lax
from jax.experimental import pallas as pl
from jax.experimental.pallas import tpu as pltpu
from jax.sharding import PartitionSpec as P

MESH = pl.DeviceIdType.MESH
LANES = 128
F32 = jnp.float32
BF16 = jnp.bfloat16


def gelu_parts(before, hidden_grad):
    scale = math.sqrt(2.0 / math.pi)
    square = before * before
    tanh = jnp.tanh(scale * (before + 0.044715 * (square * before)))
    half = 0.5 * (1.0 + tanh)
    hidden = before * half
    slope = half + 0.5 * before * (1.0 - tanh * tanh) * (scale * (1.0 + 3 * 0.044715 * square))
    return hidden.astype(BF16), (hidden_grad * slope).astype(BF16)


def dot(left, right):
    return jnp.dot(left, right, preferred_element_type=F32)


def dot_transposed(left, right):
    return lax.dot_general(left, right, (((1,), (1,)), ((), ())), preferred_element_type=F32)


def level(weights, x, g, xt, gt):
    width = weights.shape[1]
    half = width // 2
    if half % LANES == 0:
        up = weights[:, :half]
        down = weights[:, half:]
        hidden, grad = gelu_parts(dot(x, up), dot(g, down))
        term = jnp.concatenate(
            [dot(xt, grad).astype(BF16), dot(gt, hidden).astype(BF16)], axis=1
        )
        return term, dot_transposed(grad, up)
    before = dot(x, weights)
    hidden_grad = pltpu.roll(dot(g, weights), half, 1)
    hidden, grad = gelu_parts(before, hidden_grad)
    first = lax.broadcasted_iota(jnp.int32, grad.shape, 1) < half
    grad = jnp.where(first, grad.astype(F32), 0.0).astype(BF16)
    hidden = jnp.where(first, hidden.astype(F32), 0.0)
    hidden = pltpu.roll(hidden, half, 1).astype(BF16)
    term = (dot(xt, grad) + dot(gt, hidden)).astype(BF16)
    return term, dot_transposed(grad, weights)


def plan(groups, members, blocks_width):
    inner = max(k for k in range(1, math.isqrt(members) + 1) if members % k == 0)
    team = math.gcd(groups, blocks_width // LANES)
    return members // inner, inner, team


def main_kernel(
    groups,
    members,
    path_row,
    tokens,
    cotangent,
    coarse_w,
    middle_w,
    fine_w,
    all_paths,
    tokens_grad,
    middle_parts,
    fine_parts,
    coarse_parts,
    path,
    middle_send,
    fine_out,
    fine_in,
    fine_send,
    coarse_line,
    coarse_send,
    coarse_block,
    middle_block,
    fine_block,
    coarse_term,
    middle_term,
    fine_term,
    coarse_terms_in,
    coarse_sums,
    coarse_sums_in,
    coarse_total,
    xt,
    gt,
    total,
    path_send,
    path_recv,
    mem_send,
    mem_recv,
    grp_send,
    grp_recv,
    line_send,
    line_recv,
    team_send,
    team_recv,
    local_sem,
):
    group = lax.axis_index("grp")
    me = lax.axis_index("mem")
    count = groups * members
    device = group * members + me
    owned = fine_w.shape[0]
    coarse_count, rows, wide = coarse_w.shape
    outer, inner, team = plan(groups, members, wide)
    size = team * inner
    columns = wide // team
    line = me // inner
    place = lax.rem(me, inner)
    slot = lax.rem(group, team)
    team_first = group - slot
    spot = slot * inner + place

    def loop(start, stop, body):
        def wrapped(step, carry):
            body(step)
            return carry

        lax.fori_loop(start, stop, wrapped, 0)

    def column_range(s):
        return pl.ds(pl.multiple_of(s * columns, LANES), columns)

    barrier = pltpu.get_barrier_semaphore()

    def anyone(step):
        other = lax.rem(device + step, count)
        return other, (other // members, lax.rem(other, members))

    def greet(step):
        _, where = anyone(step)
        pl.semaphore_signal(barrier, inc=1, device_id=where, device_id_type=MESH)

    loop(1, count, greet)
    own_columns = coarse_w.at[:, :, column_range(slot)]
    line_self = pltpu.make_async_copy(own_columns, coarse_line.at[line], local_sem.at[0])
    line_self.start()
    pl.semaphore_wait(barrier, count - 1)

    def path_copy(step, landing_own):
        other, where = anyone(step)
        return pltpu.make_async_remote_copy(
            src_ref=path_row,
            dst_ref=all_paths.at[device if landing_own else other],
            send_sem=path_send.at[other],
            recv_sem=path_recv.at[device if landing_own else other],
            device_id=where,
            device_id_type=MESH,
        )

    loop(1, count, lambda step: path_copy(step, True).start())
    all_paths[device] = path_row[...]

    def line_copy(index, source, target, step, landing_own):
        other = lax.rem(line + step, outer)
        landing = line if landing_own else other
        return pltpu.make_async_remote_copy(
            src_ref=source(other),
            dst_ref=target.at[landing],
            send_sem=line_send.at[index, other],
            recv_sem=line_recv.at[index, landing],
            device_id={"mem": other * inner + place},
            device_id_type=MESH,
        )

    first_stage = (0, lambda other: own_columns, coarse_line)
    loop(1, outer, lambda step: line_copy(*first_stage, step, True).start())

    width = tokens.shape[1]
    for start in range(0, width, LANES):
        part = slice(start, start + LANES)
        xt[part, :] = tokens[:, part].T
        gt[part, :] = cotangent[:, part].T

    def path_done(step):
        done = path_copy(step, False)
        done.wait_recv()
        done.wait_send()

    loop(1, count, path_done)
    scalars = pltpu.make_async_copy(all_paths, path, local_sem.at[1])
    scalars.start()
    scalars.wait()

    def route(document, column):
        return path[document, 0, column]

    def member_copy(index, source, target, p, landing_own):
        landing = me if landing_own else p
        return pltpu.make_async_remote_copy(
            src_ref=source.at[p],
            dst_ref=target.at[landing],
            send_sem=mem_send.at[index, p],
            recv_sem=mem_recv.at[index, landing],
            device_id={"mem": p},
            device_id_type=MESH,
        )

    def spread(index, source, target):
        loop(
            1,
            members,
            lambda step: member_copy(
                index, source, target, lax.rem(me + step, members), True
            ).start(),
        )

    def arrive(index, source, target):
        loop(
            1,
            members,
            lambda step: member_copy(
                index, source, target, lax.rem(me + members - step, members), False
            ).wait_recv(),
        )

    def left(index, source, target):
        loop(
            1,
            members,
            lambda step: member_copy(
                index, source, target, lax.rem(me + step, members), False
            ).wait_send(),
        )

    def group_copy(index, source, target, step, landing_own):
        other = lax.rem(group + step, groups)
        landing = group if landing_own else other
        return pltpu.make_async_remote_copy(
            src_ref=source(other),
            dst_ref=target.at[landing],
            send_sem=grp_send.at[index, other],
            recv_sem=grp_recv.at[index, landing],
            device_id={"grp": other},
            device_id_type=MESH,
        )

    def group_spread(*what):
        loop(1, groups, lambda step: group_copy(*what, step, True).start())

    def group_arrive(*what):
        loop(1, groups, lambda step: group_copy(*what, step, False).wait_recv())

    def group_left(*what):
        loop(1, groups, lambda step: group_copy(*what, step, False).wait_send())

    def team_copy(index, source, target, step, landing_own):
        other = lax.rem(spot + step, size)
        landing = spot if landing_own else other
        return pltpu.make_async_remote_copy(
            src_ref=source(other),
            dst_ref=target(landing),
            send_sem=team_send.at[index, other],
            recv_sem=team_recv.at[index, landing],
            device_id=(team_first + other // inner, line * inner + lax.rem(other, inner)),
            device_id_type=MESH,
        )

    def team_document(t):
        return (team_first + t // inner) * members + line * inner + lax.rem(t, inner)

    def pick_fine(index):
        held = jnp.clip(route(index, 2) - group * owned, 0, owned - 1)
        fine_out[index // members, lax.rem(index, members)] = fine_w[held]

    def pick_middle(p):
        middle_send[p] = middle_w[route(group * members + p, 1)]

    loop(0, count, pick_fine)
    fine_trade = (0, lambda other: fine_out.at[other], fine_in)
    group_spread(*fine_trade)
    loop(0, members, pick_middle)
    spread(0, middle_send, middle_block)
    fine_in[group] = fine_out[group]
    middle_block[me] = middle_send[me]

    def merge_fine(p):
        owner = route(group * members + p, 2) // owned
        fine_send[p] = fine_in[owner, p]

    group_arrive(*fine_trade)
    loop(0, members, merge_fine)
    spread(1, fine_send, fine_block)
    fine_block[me] = fine_send[me]

    line_self.wait()
    loop(1, outer, lambda step: line_copy(*first_stage, step, False).wait_recv())

    def pick_coarse(t):
        identity = route(team_document(t), 0)
        for z in range(outer):
            coarse_send[t, z] = coarse_line[z, identity]

    loop(0, size, pick_coarse)

    def piece_of(ref, t, s):
        return ref.at[:, lax.rem(t, inner), :, column_range(s)]

    second_stage = (
        0,
        lambda other: coarse_send.at[other],
        lambda landing: piece_of(coarse_block, landing, landing // inner),
    )
    loop(1, size, lambda step: team_copy(*second_stage, step, True).start())
    block_self = pltpu.make_async_copy(
        coarse_send.at[spot], piece_of(coarse_block, place, slot), local_sem.at[2]
    )
    block_self.start()

    def compute(block, term):
        weights = block[...].reshape(width, block.shape[-1])
        value, part = level(weights, tokens[...], cotangent[...], xt[...], gt[...])
        term[...] = value.reshape(term.shape)
        return part

    middle_own = middle_parts.at[group]
    fine_own = fine_parts.at[group]

    loop(1, size, lambda step: team_copy(*second_stage, step, False).wait_recv())
    block_self.wait()
    total[...] = compute(coarse_block, coarse_term)
    gather_terms = (
        1,
        lambda other: piece_of(coarse_term, other, other // inner),
        lambda landing: coarse_terms_in.at[landing],
    )
    loop(1, size, lambda step: team_copy(*gather_terms, step, True).start())
    term_self = pltpu.make_async_copy(
        piece_of(coarse_term, place, slot), coarse_terms_in.at[spot], local_sem.at[3]
    )
    term_self.start()

    arrive(0, middle_send, middle_block)
    total[...] += compute(middle_block, middle_term)
    spread(2, middle_term, middle_own)
    middle_parts[group, me] = middle_term[me]

    arrive(1, fine_send, fine_block)
    part = compute(fine_block, fine_term)
    spread(3, fine_term, fine_own)
    fine_parts[group, me] = fine_term[me]
    tokens_grad[...] = (total[...] + part).astype(BF16)

    loop(1, size, lambda step: team_copy(*gather_terms, step, False).wait_recv())
    term_self.wait()
    step_rows = min(rows, 16)
    weight = [
        [jnp.where(route(team_document(t), 0) == k, 1.0, 0.0) for k in range(coarse_count)]
        for t in range(size)
    ]

    def add_terms(index):
        z = index // (rows // step_rows)
        some = pl.ds(pl.multiple_of(lax.rem(index, rows // step_rows) * step_rows, step_rows), step_rows)
        pieces = [coarse_terms_in[t, z, some, :].astype(F32) for t in range(size)]
        for k in range(coarse_count):
            value = pieces[0] * weight[0][k]
            for t in range(1, size):
                value = value + pieces[t] * weight[t][k]
            coarse_sums[z, k, some, :] = value.astype(BF16)

    loop(0, outer * (rows // step_rows), add_terms)
    sum_stage = (1, lambda other: coarse_sums.at[other], coarse_sums_in)
    loop(1, outer, lambda step: line_copy(*sum_stage, step, True).start())
    coarse_sums_in[line] = coarse_sums[line]

    arrive(2, middle_term, middle_own)
    middle_trade = (1, lambda other: middle_own, middle_parts)
    group_spread(*middle_trade)
    arrive(3, fine_term, fine_own)
    fine_trade_back = (2, lambda other: fine_own, fine_parts)
    group_spread(*fine_trade_back)

    left(0, middle_send, middle_block)
    left(1, fine_send, fine_block)
    group_left(*fine_trade)
    loop(1, outer, lambda step: line_copy(*first_stage, step, False).wait_send())
    loop(1, size, lambda step: team_copy(*second_stage, step, False).wait_send())
    loop(1, size, lambda step: team_copy(*gather_terms, step, False).wait_send())
    left(2, middle_term, middle_own)
    left(3, fine_term, fine_own)

    loop(1, outer, lambda step: line_copy(*sum_stage, step, False).wait_recv())
    value = coarse_sums_in[0].astype(F32)
    for z in range(1, outer):
        value = value + coarse_sums_in[z].astype(F32)
    coarse_total[...] = value.astype(BF16)
    coarse_trade = (3, lambda other: coarse_total, coarse_parts)
    group_spread(*coarse_trade)
    coarse_parts[group] = coarse_total[...]
    loop(1, outer, lambda step: line_copy(*sum_stage, step, False).wait_send())
    for trade in (middle_trade, fine_trade_back, coarse_trade):
        group_arrive(*trade)
        group_left(*trade)


def exchange(path, tokens, cotangent, coarse_w, middle_w, fine_w, groups, members):
    blocks, rows, wide = coarse_w.shape
    medium, narrow = middle_w.shape[2], fine_w.shape[2]
    token_count, width = tokens.shape
    count = groups * members
    outer, inner, team = plan(groups, members, wide)
    columns = wide // team
    size = team * inner

    def stack(*shape):
        return pltpu.VMEM(shape, BF16)

    def sems(*shape):
        return pltpu.SemaphoreType.DMA(shape)

    vmem = pl.BlockSpec(memory_space=pltpu.VMEM)
    return pl.pallas_call(
        functools.partial(main_kernel, groups, members),
        out_shape=(
            jax.ShapeDtypeStruct((count,) + path.shape, jnp.int32),
            jax.ShapeDtypeStruct(tokens.shape, BF16),
            jax.ShapeDtypeStruct((groups, members, rows, medium), BF16),
            jax.ShapeDtypeStruct((groups, members, rows, narrow), BF16),
            jax.ShapeDtypeStruct((groups, blocks, rows, columns), BF16),
        ),
        in_specs=[vmem] * 6,
        out_specs=(vmem,) * 5,
        scratch_shapes=[
            pltpu.SMEM((count,) + path.shape, jnp.int32),
            stack(members, rows, medium),
            stack(groups, members, rows, narrow),
            stack(groups, members, rows, narrow),
            stack(members, rows, narrow),
            stack(outer, blocks, rows, columns),
            stack(size, outer, rows, columns),
            stack(outer, inner, rows, wide),
            stack(members, rows, medium),
            stack(members, rows, narrow),
            stack(outer, inner, rows, wide),
            stack(members, rows, medium),
            stack(members, rows, narrow),
            stack(size, outer, rows, columns),
            stack(outer, blocks, rows, columns),
            stack(outer, blocks, rows, columns),
            stack(blocks, rows, columns),
            stack(width, token_count),
            stack(width, token_count),
            pltpu.VMEM((token_count, width), F32),
            sems(count),
            sems(count),
            sems(4, members),
            sems(4, members),
            sems(4, groups),
            sems(4, groups),
            sems(2, outer),
            sems(2, outer),
            sems(2, size),
            sems(2, size),
            sems(4),
        ],
        compiler_params=pltpu.CompilerParams(
            collective_id=0, has_side_effects=True, vmem_limit_bytes=60 * 2**20
        ),
        name="exchange",
    )(path, tokens, cotangent, coarse_w, middle_w, fine_w)


def collect_kernel(
    path,
    first_owned,
    middle_parts,
    fine_parts,
    coarse_parts,
    coarse_grad,
    middle_grad,
    fine_grad,
    middle_sum,
    fine_sum,
):
    owned = fine_grad.shape[0]
    middle_sum[...] = jnp.zeros_like(middle_sum)
    fine_sum[...] = jnp.zeros_like(fine_sum)

    def add(document, carry):
        k = path[document, 0, 1]
        middle_sum[k] += middle_parts[document].astype(F32)
        place = path[document, 0, 2] - first_owned[0]

        @pl.when((place >= 0) & (place < owned))
        def _():
            fine_sum[place] += fine_parts[document].astype(F32)

        return carry

    lax.fori_loop(0, middle_parts.shape[0], add, 0)
    middle_grad[...] = middle_sum[...].astype(BF16)
    fine_grad[...] = fine_sum[...].astype(BF16)
    groups, _, _, columns = coarse_parts.shape
    team = coarse_grad.shape[2] // columns
    for s in range(team):
        value = coarse_parts[s].astype(F32)
        for other in range(s + team, groups, team):
            value = value + coarse_parts[other].astype(F32)
        coarse_grad[:, :, s * columns : (s + 1) * columns] = value.astype(BF16)


def collect(paths, first_owned, middle_parts, fine_parts, coarse_parts, shapes):
    vmem = pl.BlockSpec(memory_space=pltpu.VMEM)
    smem = pl.BlockSpec(memory_space=pltpu.SMEM)
    return pl.pallas_call(
        collect_kernel,
        out_shape=tuple(jax.ShapeDtypeStruct(shape, BF16) for shape in shapes),
        in_specs=[smem, smem] + [vmem] * 3,
        out_specs=(vmem,) * 3,
        scratch_shapes=[pltpu.VMEM(shapes[1], F32), pltpu.VMEM(shapes[2], F32)],
        compiler_params=pltpu.CompilerParams(vmem_limit_bytes=60 * 2**20),
        name="collect",
    )(paths, first_owned, middle_parts, fine_parts, coarse_parts)


def on_device(tokens, cotangent, path, coarse_weights, middle_weights, fine_weights):
    members = lax.axis_size("mem")
    groups = lax.axis_size("grp")
    paths, tokens_grad, middle_parts, fine_parts, coarse_parts = exchange(
        path, tokens, cotangent, coarse_weights, middle_weights, fine_weights, groups, members
    )
    first_owned = (lax.axis_index("grp") * fine_weights.shape[0]).astype(jnp.int32).reshape(1)
    flat = lambda parts: parts.reshape((groups * members,) + parts.shape[2:])
    grads = collect(
        paths,
        first_owned,
        flat(middle_parts),
        flat(fine_parts),
        coarse_parts,
        (coarse_weights.shape, middle_weights.shape, fine_weights.shape),
    )
    return (tokens_grad,) + tuple(grads)


def solution(mesh):
    return jax.shard_map(
        on_device,
        mesh=mesh,
        in_specs=(
            P(("grp", "mem"), None),
            P(("grp", "mem"), None),
            P(("grp", "mem"), None),
            P(None, "mem", None),
            P(None, "mem", None),
            P("grp", "mem", None),
        ),
        out_specs=(
            P(("grp", "mem"), None),
            P(None, "mem", None),
            P(None, "mem", None),
            P("grp", "mem", None),
        ),
        check_vma=False,
    )
```

time: 120 us -> 95 us (0.79)
  Pallas kernels: 115 us -> 91.6 us
  local copies, waits for them, and re-layouts: 3.25 us -> 1.67 us
    pallas_call x1, Pallas kernels: 101 us -> 87.4 us  [exchange(): pl.pallas_call(functools.partial(main_kernel, groups, members), out_shape...]
    pallas_call x1 -> x0, Pallas kernels: 9.55 us -> none  [gather_paths(): pl.pallas_call(functools.partial(path_kernel, groups, members), out_shape...]
where the time goes in v2:
time: 95 us; the launch traced here: 93.9 us
  Pallas kernels  91.6 us (96%)
  local copies, waits for them, and re-layouts  1.67 us (2%)
    pallas_call x1, Pallas kernels, exchange(): pl.pallas_call(functools.partial(main_kernel, groups, members), out_shape...  87.4 us
    pallas_call x1, Pallas kernels, collect(): pl.pallas_call(collect_kernel, out_shape=tuple((jax.ShapeDtypeStruct(shap...  4.15 us

profile of v2, /device:TPU:11, one launch (start us, length us, event | category | flops | bytes accessed | tf_op | source)
XLA Modules:
  0.0 93.9 jit_solution(4524560425812723006)
XLA Ops:
  0.6 87.4 %exchange.1 = (s32[32,1,3]{2,1,0:T(1,128)}, bf16[128,1024]{1,0:T(8,128)(2,1)}, bf16[2,16,64,256]{3,2,1,0:T(8,128)(2,1)}, bf16[2,16,64,128]{3,2,1,0:T(8,128)(2,1)}, bf16[2,4,64,256]{3,2,1,0:T(8,128)(2,1)}) custom-call(s32[1,3]{1,0:T(1,128)} %path_row.1, bf16[128,1024]{1,0:T(8,128)(2,1)} %tokens.1, bf16[128,1024]{1,0:T(8,128)(2,1)} %cotangent.1, ...), custom_call_target="tpu_custom_call" | custom-call | tf_op jit(solution)/shard_map/exchange/pallas_call | solution.py:423
  88.1 4.2 %collect.1 = (bf16[4,64,512]{2,1,0:T(8,128)(2,1)}, bf16[64,64,256]{2,1,0:T(8,128)(2,1)}, bf16[32,64,128]{2,1,0:T(8,128)(2,1)}) custom-call(s32[32,1,3]{2,1,0:T(1,128)} %get-tuple-element.13.path, s32[1]{0:T(128)} %bitcast.first_owned, bf16[32,64,256]{2,1,0:T(8,128)(2,1)} %bitcast.3, bf16[32,64,128]{2,1,0:T(8,128)(2,1)} %bitcast.4, ...), custom_call_target="tpu_custom_call" | custom-call | tf_op jit(solution)/shard_map/collect/pallas_call | solution.py:516
  92.2 1.7 %copy.11 = bf16[128,1024]{1,0:T(8,128)(2,1)} copy(bf16[128,1024]{1,0:T(8,128)(2,1)} %get-tuple-element.24) | data formatting | bytes 524288

commit v3 on v2

--- a/solution.py
+++ b/solution.py
@@ -64,17 +64,22 @@
     groups,
     members,
     path_row,
-    tokens,
-    cotangent,
-    coarse_w,
-    middle_w,
-    fine_w,
+    tokens_hbm,
+    cotangent_hbm,
+    coarse_hbm,
+    middle_hbm,
+    fine_hbm,
     all_paths,
     tokens_grad,
     middle_parts,
     fine_parts,
     coarse_parts,
     path,
+    tokens,
+    cotangent,
+    coarse_w,
+    middle_w,
+    fine_w,
     middle_send,
     fine_out,
     fine_in,
@@ -105,6 +110,11 @@
     team_send,
     team_recv,
     local_sem,
+    load_sem,
+    middle_send_on,
+    middle_recv_on,
+    fine_send_on,
+    fine_recv_on,
 ):
     group = lax.axis_index("grp")
     me = lax.axis_index("mem")
@@ -131,6 +141,20 @@
     def column_range(s):
         return pl.ds(pl.multiple_of(s * columns, LANES), columns)
 
+    loads = [
+        pltpu.make_async_copy(source, target, load_sem.at[index])
+        for index, (source, target) in enumerate(
+            (
+                (coarse_hbm, coarse_w),
+                (fine_hbm, fine_w),
+                (middle_hbm, middle_w),
+                (tokens_hbm, tokens),
+                (cotangent_hbm, cotangent),
+            )
+        )
+    ]
+    for load in loads:
+        load.start()
     barrier = pltpu.get_barrier_semaphore()
 
     def anyone(step):
@@ -143,6 +167,7 @@
 
     loop(1, count, greet)
     own_columns = coarse_w.at[:, :, column_range(slot)]
+    loads[0].wait()
     line_self = pltpu.make_async_copy(own_columns, coarse_line.at[line], local_sem.at[0])
     line_self.start()
     pl.semaphore_wait(barrier, count - 1)
@@ -176,6 +201,8 @@
     first_stage = (0, lambda other: own_columns, coarse_line)
     loop(1, outer, lambda step: line_copy(*first_stage, step, True).start())
 
+    for load in loads[1:]:
+        load.wait()
     width = tokens.shape[1]
     for start in range(0, width, LANES):
         part = slice(start, start + LANES)
@@ -351,6 +378,43 @@
     fine_parts[group, me] = fine_term[me]
     tokens_grad[...] = (total[...] + part).astype(BF16)
 
+    def hand_on(target, send_on, recv_on, p, step, landing_own):
+        other = lax.rem(group + step, groups)
+        landing = group if landing_own else other
+        return pltpu.make_async_remote_copy(
+            src_ref=target.at[group, p],
+            dst_ref=target.at[landing, p],
+            send_sem=send_on.at[other, p],
+            recv_sem=recv_on.at[landing, p],
+            device_id={"grp": other},
+            device_id_type=MESH,
+        )
+
+    def relay(index, source, target, send_on, recv_on):
+        own = target.at[group]
+
+        def start(p):
+            loop(1, groups, lambda step: hand_on(target, send_on, recv_on, p, step, True).start())
+
+        def body(step):
+            p = lax.rem(me + members - step, members)
+            member_copy(index, source, own, p, False).wait_recv()
+            start(p)
+
+        start(me)
+        loop(1, members, body)
+
+    def relay_done(target, send_on, recv_on):
+        def body(index):
+            p = index // (groups - 1)
+            step = lax.rem(index, groups - 1) + 1
+            done = hand_on(target, send_on, recv_on, p, step, False)
+            done.wait_recv()
+            done.wait_send()
+
+        if groups > 1:
+            loop(0, members * (groups - 1), body)
+
     loop(1, size, lambda step: team_copy(*gather_terms, step, False).wait_recv())
     term_self.wait()
     step_rows = min(rows, 16)
@@ -373,13 +437,9 @@
     sum_stage = (1, lambda other: coarse_sums.at[other], coarse_sums_in)
     loop(1, outer, lambda step: line_copy(*sum_stage, step, True).start())
     coarse_sums_in[line] = coarse_sums[line]
-
-    arrive(2, middle_term, middle_own)
-    middle_trade = (1, lambda other: middle_own, middle_parts)
-    group_spread(*middle_trade)
-    arrive(3, fine_term, fine_own)
-    fine_trade_back = (2, lambda other: fine_own, fine_parts)
-    group_spread(*fine_trade_back)
+    relay(2, middle_term, middle_parts, middle_send_on, middle_recv_on)
+    relay(3, fine_term, fine_parts, fine_send_on, fine_recv_on)
+
 
     left(0, middle_send, middle_block)
     left(1, fine_send, fine_block)
@@ -395,13 +455,14 @@
     for z in range(1, outer):
         value = value + coarse_sums_in[z].astype(F32)
     coarse_total[...] = value.astype(BF16)
-    coarse_trade = (3, lambda other: coarse_total, coarse_parts)
+    coarse_trade = (1, lambda other: coarse_total, coarse_parts)
     group_spread(*coarse_trade)
     coarse_parts[group] = coarse_total[...]
     loop(1, outer, lambda step: line_copy(*sum_stage, step, False).wait_send())
-    for trade in (middle_trade, fine_trade_back, coarse_trade):
-        group_arrive(*trade)
-        group_left(*trade)
+    group_arrive(*coarse_trade)
+    group_left(*coarse_trade)
+    relay_done(middle_parts, middle_send_on, middle_recv_on)
+    relay_done(fine_parts, fine_send_on, fine_recv_on)
 
 
 def exchange(path, tokens, cotangent, coarse_w, middle_w, fine_w, groups, members):
@@ -429,10 +490,15 @@
             jax.ShapeDtypeStruct((groups, members, rows, narrow), BF16),
             jax.ShapeDtypeStruct((groups, blocks, rows, columns), BF16),
         ),
-        in_specs=[vmem] * 6,
+        in_specs=[vmem] + [pl.BlockSpec(memory_space=pl.ANY)] * 5,
         out_specs=(vmem,) * 5,
         scratch_shapes=[
             pltpu.SMEM((count,) + path.shape, jnp.int32),
+            stack(*tokens.shape),
+            stack(*cotangent.shape),
+            stack(*coarse_w.shape),
+            stack(*middle_w.shape),
+            stack(*fine_w.shape),
             stack(members, rows, medium),
             stack(groups, members, rows, narrow),
             stack(groups, members, rows, narrow),
@@ -456,13 +522,18 @@
             sems(count),
             sems(4, members),
             sems(4, members),
-            sems(4, groups),
-            sems(4, groups),
+            sems(2, groups),
+            sems(2, groups),
             sems(2, outer),
             sems(2, outer),
             sems(2, size),
             sems(2, size),
             sems(4),
+            sems(5),
+            sems(groups, members),
+            sems(groups, members),
+            sems(groups, members),
+            sems(groups, members),
         ],
         compiler_params=pltpu.CompilerParams(
             collective_id=0, has_side_effects=True, vmem_limit_bytes=60 * 2**20
@@ -474,33 +545,42 @@
 def collect_kernel(
     path,
     first_owned,
-    middle_parts,
-    fine_parts,
+    tokens_in,
+    middle_hbm,
+    fine_hbm,
     coarse_parts,
+    tokens_grad,
     coarse_grad,
     middle_grad,
     fine_grad,
+    middle_parts,
+    fine_parts,
     middle_sum,
     fine_sum,
+    middle_last,
+    fine_last,
+    load_sem,
 ):
+    count = middle_parts.shape[0]
     owned = fine_grad.shape[0]
-    middle_sum[...] = jnp.zeros_like(middle_sum)
-    fine_sum[...] = jnp.zeros_like(fine_sum)
-
-    def add(document, carry):
-        k = path[document, 0, 1]
-        middle_sum[k] += middle_parts[document].astype(F32)
-        place = path[document, 0, 2] - first_owned[0]
-
-        @pl.when((place >= 0) & (place < owned))
-        def _():
-            fine_sum[place] += fine_parts[document].astype(F32)
-
-        return carry
-
-    lax.fori_loop(0, middle_parts.shape[0], add, 0)
-    middle_grad[...] = middle_sum[...].astype(BF16)
-    fine_grad[...] = fine_sum[...].astype(BF16)
+    loads = (
+        pltpu.make_async_copy(middle_hbm, middle_parts, load_sem.at[0]),
+        pltpu.make_async_copy(fine_hbm, fine_parts, load_sem.at[1]),
+    )
+    for load in loads:
+        load.start()
+    middle_grad[...] = jnp.zeros_like(middle_grad)
+    fine_grad[...] = jnp.zeros_like(fine_grad)
+    middle_sum[count] = jnp.zeros(middle_sum.shape[1:], F32)
+    fine_sum[count] = jnp.zeros(fine_sum.shape[1:], F32)
+    for last in (middle_last, fine_last):
+
+        def clear(k, carry, last=last):
+            last[k] = count
+            return carry
+
+        lax.fori_loop(0, last.shape[0], clear, 0)
+    tokens_grad[...] = tokens_in[...]
     groups, _, _, columns = coarse_parts.shape
     team = coarse_grad.shape[2] // columns
     for s in range(team):
@@ -508,20 +588,54 @@
         for other in range(s + team, groups, team):
             value = value + coarse_parts[other].astype(F32)
         coarse_grad[:, :, s * columns : (s + 1) * columns] = value.astype(BF16)
-
-
-def collect(paths, first_owned, middle_parts, fine_parts, coarse_parts, shapes):
+    for load in loads:
+        load.wait()
+
+    def add(document, carry):
+        k = path[document, 0, 1]
+        value = middle_parts[document].astype(F32) + middle_sum[middle_last[k]]
+        middle_sum[document] = value
+        middle_grad[k] = value.astype(BF16)
+        middle_last[k] = document
+        place = path[document, 0, 2] - first_owned[0]
+
+        @pl.when((place >= 0) & (place < owned))
+        def _():
+            piece = fine_parts[document].astype(F32) + fine_sum[fine_last[place]]
+            fine_sum[document] = piece
+            fine_grad[place] = piece.astype(BF16)
+            fine_last[place] = document
+
+        return carry
+
+    lax.fori_loop(0, count, add, 0)
+
+
+def collect(paths, first_owned, tokens_grad, middle_parts, fine_parts, coarse_parts, shapes):
     vmem = pl.BlockSpec(memory_space=pltpu.VMEM)
     smem = pl.BlockSpec(memory_space=pltpu.SMEM)
+    hbm = pl.BlockSpec(memory_space=pl.ANY)
+    count, rows, medium = middle_parts.shape
+    narrow = fine_parts.shape[2]
     return pl.pallas_call(
         collect_kernel,
-        out_shape=tuple(jax.ShapeDtypeStruct(shape, BF16) for shape in shapes),
-        in_specs=[smem, smem] + [vmem] * 3,
-        out_specs=(vmem,) * 3,
-        scratch_shapes=[pltpu.VMEM(shapes[1], F32), pltpu.VMEM(shapes[2], F32)],
+        out_shape=tuple(
+            jax.ShapeDtypeStruct(shape, BF16) for shape in (tokens_grad.shape,) + shapes
+        ),
+        in_specs=[smem, smem, vmem, hbm, hbm, vmem],
+        out_specs=(vmem,) * 4,
+        scratch_shapes=[
+            pltpu.VMEM(middle_parts.shape, BF16),
+            pltpu.VMEM(fine_parts.shape, BF16),
+            pltpu.VMEM((count + 1, rows, medium), F32),
+            pltpu.VMEM((count + 1, rows, narrow), F32),
+            pltpu.SMEM((shapes[1][0],), jnp.int32),
+            pltpu.SMEM((shapes[2][0],), jnp.int32),
+            pltpu.SemaphoreType.DMA((2,)),
+        ],
         compiler_params=pltpu.CompilerParams(vmem_limit_bytes=60 * 2**20),
         name="collect",
-    )(paths, first_owned, middle_parts, fine_parts, coarse_parts)
+    )(paths, first_owned, tokens_grad, middle_parts, fine_parts, coarse_parts)
 
 
 def on_device(tokens, cotangent, path, coarse_weights, middle_weights, fine_weights):
@@ -532,15 +646,15 @@
     )
     first_owned = (lax.axis_index("grp") * fine_weights.shape[0]).astype(jnp.int32).reshape(1)
     flat = lambda parts: parts.reshape((groups * members,) + parts.shape[2:])
-    grads = collect(
+    return collect(
         paths,
         first_owned,
+        tokens_grad,
         flat(middle_parts),
         flat(fine_parts),
         coarse_parts,
         (coarse_weights.shape, middle_weights.shape, fine_weights.shape),
     )
-    return (tokens_grad,) + tuple(grads)
 
 
 def solution(mesh):

time: 95 us -> 92.7 us (0.976)
  local copies, waits for them, and re-layouts: 1.67 us -> 0 us
    unnamed x1 -> x0, local copies, waits for them, and re-layouts: 1.67 us -> none
where the time goes in v3:
time: 92.7 us; the launch traced here: 92.5 us
  Pallas kernels  91.8 us (99%)
    pallas_call x1, Pallas kernels, exchange(): pl.pallas_call(functools.partial(main_kernel, groups, members), out_shape...  86.9 us
    pallas_call x1, Pallas kernels, collect(): pl.pallas_call(collect_kernel, out_shape=tuple((jax.ShapeDtypeStruct(shap...  4.88 us

profile of v3, /device:TPU:11, one launch (start us, length us, event | category | flops | bytes accessed | tf_op | source)
XLA Modules:
  0.0 92.5 jit_solution(1992238970520036511)
XLA Ops:
  0.6 86.9 %exchange.1 = (s32[32,1,3]{2,1,0:T(1,128)}, bf16[128,1024]{1,0:T(8,128)(2,1)}, bf16[2,16,64,256]{3,2,1,0:T(8,128)(2,1)}, bf16[2,16,64,128]{3,2,1,0:T(8,128)(2,1)}, bf16[2,4,64,256]{3,2,1,0:T(8,128)(2,1)}) custom-call(s32[1,3]{1,0:T(1,128)} %path_row.1, bf16[128,1024]{1,0:T(8,128)(2,1)} %tokens_hbm.1, bf16[128,1024]{1,0:T(8,128)(2,1)} %cotangent_hbm.1, ...), custom_call_target="tpu_custom_call" | custom-call | tf_op jit(solution)/shard_map/exchange/pallas_call | solution.py:484
  87.6 4.9 %collect.1 = (bf16[128,1024]{1,0:T(8,128)(2,1)}, bf16[4,64,512]{2,1,0:T(8,128)(2,1)}, bf16[64,64,256]{2,1,0:T(8,128)(2,1)}, bf16[32,64,128]{2,1,0:T(8,128)(2,1)}) custom-call(s32[32,1,3]{2,1,0:T(1,128)} %get-tuple-element.9.path, s32[1]{0:T(128)} %bitcast.first_owned, bf16[128,1024]{1,0:T(8,128)(2,1)} %get-tuple-element.10.tokens_in, ...), custom_call_target="tpu_custom_call" | custom-call | tf_op jit(solution)/shard_map/collect/pallas_call | solution.py:620

commit v4 on v3

--- a/solution.py
+++ b/solution.py
@@ -353,9 +353,14 @@
     middle_own = middle_parts.at[group]
     fine_own = fine_parts.at[group]
 
+    arrive(0, middle_send, middle_block)
+    total[...] = compute(middle_block, middle_term)
+    spread(2, middle_term, middle_own)
+    middle_parts[group, me] = middle_term[me]
+
     loop(1, size, lambda step: team_copy(*second_stage, step, False).wait_recv())
     block_self.wait()
-    total[...] = compute(coarse_block, coarse_term)
+    total[...] += compute(coarse_block, coarse_term)
     gather_terms = (
         1,
         lambda other: piece_of(coarse_term, other, other // inner),
@@ -366,11 +371,6 @@
         piece_of(coarse_term, place, slot), coarse_terms_in.at[spot], local_sem.at[3]
     )
     term_self.start()
-
-    arrive(0, middle_send, middle_block)
-    total[...] += compute(middle_block, middle_term)
-    spread(2, middle_term, middle_own)
-    middle_parts[group, me] = middle_term[me]
 
     arrive(1, fine_send, fine_block)
     part = compute(fine_block, fine_term)
@@ -415,6 +415,8 @@
         if groups > 1:
             loop(0, members * (groups - 1), body)
 
+    relay(2, middle_term, middle_parts, middle_send_on, middle_recv_on)
+
     loop(1, size, lambda step: team_copy(*gather_terms, step, False).wait_recv())
     term_self.wait()
     step_rows = min(rows, 16)
@@ -437,7 +439,6 @@
     sum_stage = (1, lambda other: coarse_sums.at[other], coarse_sums_in)
     loop(1, outer, lambda step: line_copy(*sum_stage, step, True).start())
     coarse_sums_in[line] = coarse_sums[line]
-    relay(2, middle_term, middle_parts, middle_send_on, middle_recv_on)
     relay(3, fine_term, fine_parts, fine_send_on, fine_recv_on)
 
 

time: 92.7 us -> 87.8 us (0.947)
  Pallas kernels: 91.8 us -> 87 us
    pallas_call x1, Pallas kernels: 86.9 us -> 82.1 us  [exchange(): pl.pallas_call(functools.partial(main_kernel, groups, members), out_shape...]
where the time goes in v4:
time: 87.8 us; the launch traced here: 87.6 us
  Pallas kernels  87 us (99%)
    pallas_call x1, Pallas kernels, exchange(): pl.pallas_call(functools.partial(main_kernel, groups, members), out_shape...  82.1 us
    pallas_call x1, Pallas kernels, collect(): pl.pallas_call(collect_kernel, out_shape=tuple((jax.ShapeDtypeStruct(shap...  4.9 us

profile of v4, /device:TPU:11, one launch (start us, length us, event | category | flops | bytes accessed | tf_op | source)
XLA Modules:
  0.0 87.6 jit_solution(14254881850600471613)
XLA Ops:
  0.6 82.1 %exchange.1 = (s32[32,1,3]{2,1,0:T(1,128)}, bf16[128,1024]{1,0:T(8,128)(2,1)}, bf16[2,16,64,256]{3,2,1,0:T(8,128)(2,1)}, bf16[2,16,64,128]{3,2,1,0:T(8,128)(2,1)}, bf16[2,4,64,256]{3,2,1,0:T(8,128)(2,1)}) custom-call(s32[1,3]{1,0:T(1,128)} %path_row.1, bf16[128,1024]{1,0:T(8,128)(2,1)} %tokens_hbm.1, bf16[128,1024]{1,0:T(8,128)(2,1)} %cotangent_hbm.1, ...), custom_call_target="tpu_custom_call" | custom-call | tf_op jit(solution)/shard_map/exchange/pallas_call | solution.py:485
  82.7 4.9 %collect.1 = (bf16[128,1024]{1,0:T(8,128)(2,1)}, bf16[4,64,512]{2,1,0:T(8,128)(2,1)}, bf16[64,64,256]{2,1,0:T(8,128)(2,1)}, bf16[32,64,128]{2,1,0:T(8,128)(2,1)}) custom-call(s32[32,1,3]{2,1,0:T(1,128)} %get-tuple-element.9.path, s32[1]{0:T(128)} %bitcast.first_owned, bf16[128,1024]{1,0:T(8,128)(2,1)} %get-tuple-element.10.tokens_in, ...), custom_call_target="tpu_custom_call" | custom-call | tf_op jit(solution)/shard_map/collect/pallas_call | solution.py:621
